TPU v7x, 256 devices: a 4x2x16 block of a 4x16x16 slice. The times are simulated.
256 devices in a mesh: rep: 2 (over y), ep: 128 (over x, z, core).
Axes of the slice: x: 4, y: 2, z: 16, core: 2. Of those that a mesh axis runs over, the one named last changes fastest.
The devices are a block of a 4x16x16 slice.
Arguments:
- cache_kv: bfloat16 [512, 2048, 576], P(('rep', 'ep')), parts along dimension 0, may hold values from -6 to 6
- new_kv: bfloat16 [512, 2, 576], P(('rep', 'ep')), parts along dimension 0, may hold values from -6 to 6
- queries: bfloat16 [512, 2, 64, 576], P(('rep', 'ep')), parts along dimension 0, may hold values from -256 to 256
- lengths: int32 [512], P(('rep', 'ep')), parts along dimension 0, may hold values from 256 to 2048
- resid: bfloat16 [512, 2, 7168], P(('rep', 'ep')), parts along dimension 0, may hold values from -18 to 18
- value_up: bfloat16 [512, 8192], P(None, 'ep'), may hold values from -1.5 to 1.5
- out_proj: bfloat16 [8192, 7168], P('ep'), may hold values from -0.09375 to 0.09375
- norm_gain: bfloat16 [7168], replicated, may hold values from 0.25 to 1.75
- router: bfloat16 [7168, 16], replicated, may hold values from -0.0625 to 0.0625
- expert_ids: int32 [512, 2, 8], P(('rep', 'ep')), parts along dimension 0, may hold values from 0 to 15, as said below
- slots: int32 [512, 2, 8], P(('rep', 'ep')), parts along dimension 0, may hold values from 0 to 3, as said below
- w_gate: bfloat16 [7168, 16384], P(None, 'ep'), may hold values from -0.0625 to 0.0625
- w_up: bfloat16 [7168, 16384], P(None, 'ep'), may hold values from -0.0625 to 0.0625
- w_down: bfloat16 [16384, 7168], P('ep'), may hold values from -0.1875 to 0.1875
Outputs:
- mixed: bfloat16 [512, 2, 7168], P(('rep', 'ep')), parts along dimension 0
There are 2 independent parts, one for each index of `rep`. A program takes and returns all parts, laid end to end along the dimension named above; an argument that names none is the same for every part. Nothing has to cross between parts.
Inputs may be any that keep to these rules, and one draw needn't show every extreme that they name: `expert_ids`: each row names 8 different experts. In each aligned block of 4 rows (the rows of one device), the rows that name the same expert carry the distinct slots 0 up to their number minus one for it; in every block some expert is named by all 4 rows.
All inputs are finite; a program needn't handle non-finite values.
Results may differ from a plain program's by a relative error of at most 0.0065.
Values may be sent and summed in bfloat16 or wider, within the bound.
No kernel may reach another device: no remote copies, remote signals or barrier semaphores. Data moves between devices by JAX's collectives and lax.ppermute only.
A program may use at most 128 MiB of HBM per device.

v0:
```python
import math
import jax
import jax.numpy as jnp
from jax import lax
from jax.sharding import PartitionSpec as P

D = 7168
H = 64
LAT = 512
VH = 128
EXPERTS = 16
TOP = 8
CAP = 2
QK = 192
route_scale = 2.827
norm_eps = 1e-06


def softmax_parts(score_cache, score_new):
    row_peak = jnp.maximum(jnp.max(score_cache, axis=-1), jnp.max(score_new, axis=-1))
    exp_cache = jnp.exp(score_cache - row_peak[..., None])
    exp_new = jnp.exp(score_new - row_peak[..., None])
    exp_total = jnp.sum(exp_cache, axis=-1) + jnp.sum(exp_new, axis=-1)
    prob_cache = (exp_cache / exp_total[..., None]).astype(jnp.bfloat16)
    prob_new = (exp_new / exp_total[..., None]).astype(jnp.bfloat16)
    return (prob_cache, prob_new)


def attention(cache_kv, new_kv, queries, lengths):
    score_scale = 1.0 / math.sqrt(QK)
    cache_len = cache_kv.shape[1]
    step_count = new_kv.shape[1]
    score_new = (
        jnp.einsum("bshk,btk->bsht", queries, new_kv, preferred_element_type=jnp.float32)
        * score_scale
    )
    step_ids = jnp.arange(step_count, dtype=jnp.int32)
    causal = step_ids[None, :] <= step_ids[:, None]
    score_new = jnp.where(causal[None, :, None, :], score_new, -jnp.inf)
    score_cache = (
        jnp.einsum("bshk,bpk->bshp", queries, cache_kv, preferred_element_type=jnp.float32)
        * score_scale
    )
    position = jnp.arange(cache_len, dtype=jnp.int32)
    is_live = position[None, :] < lengths[:, None]
    score_cache = jnp.where(is_live[:, None, None, :], score_cache, -jnp.inf)
    prob_cache, prob_new = softmax_parts(score_cache, score_new)
    context = jnp.einsum(
        "bshp,bpc->bshc", prob_cache, cache_kv[:, :, :LAT], preferred_element_type=jnp.float32
    )
    context = context + jnp.einsum(
        "bsht,btc->bshc", prob_new, new_kv[:, :, :LAT], preferred_element_type=jnp.float32
    )
    return context.astype(jnp.bfloat16)


def expert_ffn(token_rows, w_gate, w_up, w_down):
    gate = jnp.dot(token_rows, w_gate, preferred_element_type=jnp.float32)
    upward = jnp.dot(token_rows, w_up, preferred_element_type=jnp.float32)
    act = (jax.nn.silu(gate) * upward).astype(jnp.bfloat16)
    return jnp.dot(act, w_down, preferred_element_type=jnp.float32)


def route_weights(token_rows, route_ids, router):
    logits = jnp.dot(token_rows, router, preferred_element_type=jnp.float32)
    expert_range = jnp.arange(router.shape[1], dtype=jnp.int32)
    is_pick = route_ids[:, :, None] == expert_range[None, None, :]
    picked = jnp.sum(jnp.where(is_pick, logits[:, None, :], 0.0), axis=-1)
    gates = jax.nn.sigmoid(picked)
    return route_scale * gates / jnp.sum(gates, axis=1, keepdims=True)


def body(
    cache_kv,
    new_kv,
    queries,
    lengths,
    resid,
    value_up,
    out_proj,
    norm_gain,
    router,
    expert_ids,
    slots,
    w_gate,
    w_up,
    w_down,
):
    devices = lax.axis_size("ep")
    context = attention(cache_kv, new_kv, queries, lengths)
    tok_count = context.shape[0] * context.shape[1]
    context = context.reshape(tok_count, H, LAT)
    value_cols = value_up.shape[1]
    heads_per = max(1, value_cols // VH)
    outgoing = jnp.repeat(context, VH // value_cols, axis=1)
    arrived = lax.all_to_all(outgoing, "ep", split_axis=1, concat_axis=0, tiled=True)
    value_table = value_up.reshape(LAT, heads_per, value_cols // heads_per)
    values = jnp.einsum("rhc,chv->rhv", arrived, value_table, preferred_element_type=jnp.float32)
    values = values.astype(jnp.bfloat16).reshape(devices * tok_count, value_cols)
    turned = lax.all_to_all(out_proj, "ep", split_axis=1, concat_axis=0, tiled=True)
    column_share = jnp.dot(
        lax.all_gather(values, "ep", axis=1, tiled=True), turned, preferred_element_type=jnp.float32
    )
    attended = lax.all_to_all(column_share, "ep", split_axis=0, concat_axis=1, tiled=True)
    hidden = resid.reshape(tok_count, D).astype(jnp.float32) + attended
    mean_square = jnp.mean(hidden * hidden, axis=-1, keepdims=True)
    normed = (hidden * lax.rsqrt(mean_square + norm_eps) * norm_gain.astype(jnp.float32)).astype(
        jnp.bfloat16
    )
    route_ids = expert_ids.reshape(tok_count, TOP)
    route_slots = slots.reshape(tok_count, TOP)
    group_size = devices // EXPERTS
    weights = route_weights(normed, route_ids, router)
    expert_grid = (
        route_ids[:, :, None] == jnp.arange(EXPERTS, dtype=jnp.int32)[None, None, :]
    ).astype(jnp.float32)
    slot_grid = (route_slots[:, :, None] == jnp.arange(CAP, dtype=jnp.int32)[None, None, :]).astype(
        jnp.float32
    )
    places = jnp.sum(expert_grid[:, :, :, None] * slot_grid[:, :, None, :], axis=1)
    shares = jnp.sum(
        expert_grid[:, :, :, None] * slot_grid[:, :, None, :] * weights[:, :, None, None], axis=1
    )
    places_dest = jnp.repeat(places, group_size, axis=1)
    shares_dest = jnp.repeat(shares, group_size, axis=1)
    outgoing_rows = jnp.einsum(
        "tjc,td->jcd", places_dest.astype(jnp.bfloat16), normed, preferred_element_type=jnp.float32
    ).astype(jnp.bfloat16)
    slot_rows = lax.all_to_all(outgoing_rows, "ep", split_axis=0, concat_axis=0, tiled=True)
    flat_rows = slot_rows.reshape(-1, slot_rows.shape[2])
    produced = expert_ffn(flat_rows, w_gate, w_up, w_down)
    produced = produced.reshape(slot_rows.shape[0], slot_rows.shape[1], produced.shape[1])
    returned = lax.all_to_all(
        produced.astype(jnp.bfloat16), "ep", split_axis=0, concat_axis=0, tiled=True
    ).astype(produced.dtype)
    expert_mix = jnp.dot(
        shares_dest.reshape(tok_count, devices * CAP),
        returned.reshape(devices * CAP, D),
        precision=lax.Precision.HIGHEST,
    )
    mixed = (hidden + expert_mix).astype(jnp.bfloat16)
    return mixed.reshape(resid.shape)


def solution(mesh):
    return jax.shard_map(
        body,
        mesh=mesh,
        in_specs=(
            P(("rep", "ep"), None, None),
            P(("rep", "ep"), None, None),
            P(("rep", "ep"), None, None, None),
            P(("rep", "ep")),
            P(("rep", "ep"), None, None),
            P(None, "ep"),
            P("ep", None),
            P(),
            P(),
            P(("rep", "ep"), None, None),
            P(("rep", "ep"), None, None),
            P(None, "ep"),
            P(None, "ep"),
            P("ep", None),
        ),
        out_specs=P(("rep", "ep"), None, None),
        check_vma=False,
    )
```

profile of v0, /device:TPU:164, one launch (start us, length us, event | category | flops | bytes accessed | tf_op | source)
XLA Modules:
  0.0 692.0 jit_solution(3392303585385041434)
XLA Ops:
  6.6 0.9 iota_compare_fusion.1
  7.5 3.8 fusion.41
  12.0 1.7 fusion.5
  14.4 61.0 %all_to_all.60 = bf16[4,128,512]{2,0,1:T(4,128)(2,1)S(1)} all-to-all(bf16[4,128,512]{2,0,1:T(4,128)(2,1)S(1)} %bitcast.75), channel_id=1, replica_groups=mesh['rep'=2,'ep'=128] {'ep'}, dimensions={1} | all-to-all | bytes 1048576 | tf_op jit(solution)/shard_map/all_to_all | solution.py:96
  75.6 0.9 convolution_convert_fusion.2
  76.5 2.6 copy.54
  79.2 3.4 reshape.151
  82.6 62.4 %all_to_all.61 = bf16[128,2,1792]{2,1,0:T(2,128)(2,1)} all-to-all(bf16[128,2,1792]{2,1,0:T(2,128)(2,1)S(1)} %reshape.151), channel_id=1, replica_groups=mesh['rep'=2,'ep'=128] {'ep'}, dimensions={0} | all-to-all | bytes 1835008 | tf_op jit(solution)/shard_map/all_to_all | solution.py:100
  145.0 4.3 reshape.152
  149.3 1.6 bitcast_bitcast_fusion
  151.0 1.8 copy.43
  152.7 3.0 reshape.147
  155.7 61.1 %all-gather.2.cloned.1.call-done = bf16[512,8192]{0,1:T(8,128)(2,1)} async-done(((bf16[512,64]{0,1:T(8,128)(2,1)}), bf16[512,8192]{0,1:T(8,128)(2,1)}) %all-gather.2.cloned.1.call-update) | async-done | bytes 8388624 | tf_op jit(solution)/shard_map/all_gather | solution.py:102
  216.8 11.4 %copy.41 = bf16[512,8192]{1,0:T(8,128)(2,1)} copy(bf16[512,8192]{0,1:T(8,128)(2,1)} %all-gather.2.cloned.1.call-done) | data formatting | bytes 16777216 | tf_op jit(solution)/shard_map/all_gather | solution.py:102
  228.2 13.1 %dot_general.43 = bf16[128,4,8192]{2,1,0:T(4,128)(2,1)} reshape(bf16[512,8192]{1,0:T(8,128)(2,1)} %copy.41) | data formatting | bytes 16777216 | tf_op jit(solution)/shard_map/dot_general | solution.py:101
  241.3 12.4 %fusion = f32[128,4,56]{0,2,1:T(8,128)S(1)} fusion(bf16[8192,56,1]{0,1,2:T(8,128)(2,1)S(1)} %reshape.147, bf16[128,4,8192]{2,1,0:T(4,128)(2,1)} %dot_general.43), kind=kOutput, calls=%fused_computation.2 | convolution fusion | flops 469762048 | bytes 9420800 | tf_op jit(solution)/shard_map/dot_general | solution.py:101
  253.8 0.9 reshape.153
  254.8 14.2 %all-to-all-start.2 = ((f32[128,1,224]{2,1,0:T(1,128)}), f32[128,1,224]{2,1,0:T(1,128)S(1)}, u32[]{:S(2)}, u32[]{:S(2)}) async-start(f32[128,1,224]{2,1,0:T(1,128)} %reshape.153), calls=%async_computation.2 | async-start | bytes 262144 | tf_op jit(solution)/shard_map/all_to_all | solution.py:104
  269.5 14.2 %all-to-all-done.2 = f32[128,1,224]{2,1,0:T(1,128)S(1)} async-done(((f32[128,1,224]{2,1,0:T(1,128)}), f32[128,1,224]{2,1,0:T(1,128)S(1)}, u32[]{:S(2)}, u32[]{:S(2)}) %all-to-all-start.2) | async-done | bytes 114720 | tf_op jit(solution)/shard_map/all_to_all | solution.py:104
  284.2 1.0 reduce.1
  287.0 1.2 convolution_convert_fusion.1
  288.2 3.8 copy.49
  292.0 176.9 %all_to_all.62 = bf16[128,2,7168]{2,1,0:T(2,128)(2,1)} all-to-all(bf16[128,2,7168]{2,1,0:T(2,128)(2,1)S(1)} %copy.49), channel_id=1, replica_groups=mesh['rep'=2,'ep'=128] {'ep'}, dimensions={0} | all-to-all | bytes 7340032 | tf_op jit(solution)/shard_map/all_to_all | solution.py:129
  468.9 8.4 %reshape.138 = bf16[256,7168]{1,0:T(8,128)(2,1)} reshape(bf16[128,2,7168]{2,1,0:T(2,128)(2,1)} %all_to_all.62) | data formatting | bytes 7340032 | tf_op jit(solution)/shard_map/reshape | solution.py:130
  477.3 3.7 fusion.43
  481.0 6.6 convolution_convert_fusion
  487.6 8.1 %convert_element_type.95 = bf16[128,2,7168]{2,1,0:T(2,128)(2,1)} reshape(bf16[256,7168]{1,0:T(8,128)(2,1)} %convolution_convert_fusion) | data formatting | bytes 7340032 | tf_op jit(solution)/shard_map/convert_element_type | solution.py:134
  495.7 10.9 %all-to-all-start.4 = ((bf16[128,2,7168]{2,1,0:T(2,128)(2,1)}), bf16[128,2,7168]{2,1,0:T(2,128)(2,1)}, u32[]{:S(2)}, u32[]{:S(2)}) async-start(bf16[128,2,7168]{2,1,0:T(2,128)(2,1)} %convert_element_type.95), calls=%async_computation.4 | async-start | bytes 7340032 | tf_op jit(solution)/shard_map/all_to_all | solution.py:133
  506.8 165.5 %all-to-all-done.4 = bf16[128,2,7168]{2,1,0:T(2,128)(2,1)} async-done(((bf16[128,2,7168]{2,1,0:T(2,128)(2,1)}), bf16[128,2,7168]{2,1,0:T(2,128)(2,1)}, u32[]{:S(2)}, u32[]{:S(2)}) %all-to-all-start.4) | async-done | bytes 3670048 | tf_op jit(solution)/shard_map/all_to_all | solution.py:133
  672.3 8.4 %reshape.139 = bf16[256,7168]{1,0:T(8,128)(2,1)} reshape(bf16[128,2,7168]{2,1,0:T(2,128)(2,1)} %all-to-all-done.4) | data formatting | bytes 7340032 | tf_op jit(solution)/shard_map/reshape | solution.py:138
  680.7 3.6 fusion.2
  684.3 0.7 reshape.140
  (57 shorter events, 4.6 us)
Async XLA Ops:
  6.5 474.5 %copy-start = (bf16[128,7168]{1,0:T(8,128)(2,1)S(1)}, bf16[128,7168]{1,0:T(8,128)(2,1)}, u32[]{:S(2)}) copy-start(bf16[128,7168]{1,0:T(8,128)(2,1)} %param.27) | copy-start | bytes 5505028
  6.6 210.3 %all-gather.2.cloned.1.call-start = ((), (), s32[]{:S(2)}) async-start(), calls=%async_computation.5 | async-start | bytes 8454144 | tf_op jit(solution)/shard_map/all_gather | solution.py:102
  7.4 3.8 copy-start.2
  7.4 3.8 copy-start.8
  7.5 4.6 copy-start.1
  13.8 61.8 %copy-start.5 = (bf16[512,64]{0,1:T(8,128)(2,1)S(1)}, bf16[512,64]{0,1:T(8,128)(2,1)}, u32[]{:S(2)}) copy-start(bf16[512,64]{0,1:T(8,128)(2,1)} %param.19) | copy-start | bytes 196612
  241.3 27.7 %copy-start.4 = (bf16[2,2,7168]{2,1,0:T(2,128)(2,1)S(1)}, bf16[2,2,7168]{2,1,0:T(2,128)(2,1)}, u32[]{:S(2)}) copy-start(bf16[2,2,7168]{2,1,0:T(2,128)(2,1)} %param.18) | copy-start | bytes 172036
  241.3 28.0 %copy-start.6 = (bf16[7168]{0:T(1024)(128)(2,1)S(1)}, bf16[7168]{0:T(1024)(128)(2,1)}, u32[]{:S(2)}) copy-start(bf16[7168]{0:T(1024)(128)(2,1)} %param.21) | copy-start | bytes 43012
  241.3 28.1 %copy-start.9 = (s32[2,2,8]{2,1,0:T(2,128)S(1)}, s32[2,2,8]{2,1,0:T(2,128)}, u32[]{:S(2)}) copy-start(s32[2,2,8]{2,1,0:T(2,128)} %param.24) | copy-start | bytes 388
  241.3 28.1 %copy-start.7 = (s32[2,2,8]{2,1,0:T(2,128)S(1)}, s32[2,2,8]{2,1,0:T(2,128)}, u32[]{:S(2)}) copy-start(s32[2,2,8]{2,1,0:T(2,128)} %param.23) | copy-start | bytes 388
  253.7 32.1 %copy-start.3 = (bf16[7168,16]{0,1:T(8,128)(2,1)S(1)}, bf16[7168,16]{0,1:T(8,128)(2,1)}, u32[]{:S(2)}) copy-start(bf16[7168,16]{0,1:T(8,128)(2,1)} %param.22) | copy-start | bytes 688132
  254.8 28.9 %all-to-all-start.2 = ((f32[128,1,224]{2,1,0:T(1,128)}), f32[128,1,224]{2,1,0:T(1,128)S(1)}, u32[]{:S(2)}, u32[]{:S(2)}) async-start(f32[128,1,224]{2,1,0:T(1,128)} %reshape.153), calls=%async_computation.2 | async-start | bytes 262144 | tf_op jit(solution)/shard_map/all_to_all | solution.py:104
  495.7 176.5 %all-to-all-start.4 = ((bf16[128,2,7168]{2,1,0:T(2,128)(2,1)}), bf16[128,2,7168]{2,1,0:T(2,128)(2,1)}, u32[]{:S(2)}, u32[]{:S(2)}) async-start(bf16[128,2,7168]{2,1,0:T(2,128)(2,1)} %convert_element_type.95), calls=%async_computation.4 | async-start | bytes 7340032 | tf_op jit(solution)/shard_map/all_to_all | solution.py:133
Sparse Core Ops, SparseCore 0:
  76.7 140.1 all-gather.1
where the time goes:
time: 702 us; the launch traced here: 692 us
  blocking collectives  300 us (43%)
  waiting for transfers between devices  241 us (34%)
  local copies, waits for them, and re-layouts  73.9 us (11%)
  matrix products  34.7 us (5%)
  starting transfers between devices  25.1 us (4%)
  between operations  14 us (2%)
    all_to_all x1, blocking collectives, body(): lax.all_to_all(outgoing_rows, 'ep', split_axis=0, concat_axis=0, tiled=True)  177 us
    all_to_all x1, waiting for transfers between devices, body(): lax.all_to_all(produced.astype(jnp.bfloat16), 'ep', split_axis=0, concat_...  165 us
    all_to_all x1, blocking collectives, body(): lax.all_to_all(out_proj, 'ep', split_axis=1, concat_axis=0, tiled=True)  62.4 us
    all_gather x1, waiting for transfers between devices, body(): lax.all_gather(values, 'ep', axis=1, tiled=True)  61.1 us
    all_to_all x1, blocking collectives, body(): lax.all_to_all(outgoing, 'ep', split_axis=1, concat_axis=0, tiled=True)  61 us
    all_to_all x1, waiting for transfers between devices, body(): lax.all_to_all(column_share, 'ep', split_axis=0, concat_axis=1, tiled=True)  14.2 us
    all_to_all x1, starting transfers between devices, body(): lax.all_to_all(column_share, 'ep', split_axis=0, concat_axis=1, tiled=True)  14.2 us
  transfers between devices with their start and end apart: 3, of which 3 were waited for; matrix products, arithmetic and copies ran while one was open for 2% of the time, Pallas kernels for 0%

commit v1 on v0

--- a/solution.py
+++ b/solution.py
@@ -99,7 +99,11 @@
     values = values.astype(jnp.bfloat16).reshape(devices * tok_count, value_cols)
     turned = lax.all_to_all(out_proj, "ep", split_axis=1, concat_axis=0, tiled=True)
     column_share = jnp.dot(
-        lax.all_gather(values, "ep", axis=1, tiled=True), turned, preferred_element_type=jnp.float32
+        jnp.concatenate(
+            lax.all_to_all(jnp.stack([values] * lax.axis_size("ep")), "ep", 0, 0), axis=1
+        ),
+        turned,
+        preferred_element_type=jnp.float32,
     )
     attended = lax.all_to_all(column_share, "ep", split_axis=0, concat_axis=1, tiled=True)
     hidden = resid.reshape(tok_count, D).astype(jnp.float32) + attended

time: 702 us -> 1010 us (1.44)
  waiting for transfers between devices: 241 us -> 610 us
  blocking collectives: 300 us -> 177 us
  starting transfers between devices: 25.1 us -> 73.7 us
  local copies, waits for them, and re-layouts: 73.9 us -> 103 us
  between operations: 14 us -> 0.62 us
    all_to_all x0 -> x3, waiting for transfers between devices: none -> 430 us  [the longest x1 357 us: body(): lax.all_to_all(jnp.stack([values] * lax.axis_size('ep')), 'ep', 0, 0)]
    all_to_all x2 -> x0, blocking collectives: 123 us -> none  [the longest x1 62.4 us: body(): lax.all_to_all(out_proj, 'ep', split_axis=1, concat_axis=0, tiled=True)]
    all_gather x1 -> x0, waiting for transfers between devices: 61.1 us -> none  [body(): lax.all_gather(values, 'ep', axis=1, tiled=True)]
    all_to_all x0 -> x3, starting transfers between devices: none -> 49.8 us  [the longest x1 29.4 us: body(): lax.all_to_all(outgoing, 'ep', split_axis=1, concat_axis=0, tiled=True)]
    reshape x0 -> x1, local copies, waits for them, and re-layouts: none -> 24 us  [body(): jnp.concatenate(lax.all_to_all(jnp.stack([values] * lax.axis_size('ep')),...]
    dot_general x2, local copies, waits for them, and re-layouts: 13.2 us -> 26 us  [body(): jnp.dot(jnp.concatenate(lax.all_to_all(jnp.stack([values] * lax.axis_size...]
    all_gather x1 -> x0, local copies, waits for them, and re-layouts: 11.4 us -> none  [body(): lax.all_gather(values, 'ep', axis=1, tiled=True)]
  transfers between devices with their start and end apart: 3 -> 5, of which waited for: 3 -> 5; matrix products, arithmetic and copies ran while one was open for 2% -> 2% of each run, Pallas kernels for 0% -> 0%
where the time goes in v1:
time: 1010 us; the launch traced here: 1000 us
  waiting for transfers between devices  610 us (60%)
  blocking collectives  177 us (18%)
  local copies, waits for them, and re-layouts  103 us (10%)
  starting transfers between devices  73.7 us (7%)
  matrix products  34 us (3%)
    all_to_all x1, waiting for transfers between devices, body(): lax.all_to_all(jnp.stack([values] * lax.axis_size('ep')), 'ep', 0, 0)  357 us
    all_to_all x1, blocking collectives, body(): lax.all_to_all(outgoing_rows, 'ep', split_axis=0, concat_axis=0, tiled=True)  177 us
    all_to_all x1, waiting for transfers between devices, body(): lax.all_to_all(produced.astype(jnp.bfloat16), 'ep', split_axis=0, concat_...  165 us
    all_to_all x1, waiting for transfers between devices, body(): lax.all_to_all(out_proj, 'ep', split_axis=1, concat_axis=0, tiled=True)  46.7 us
    all_to_all x1, starting transfers between devices, body(): lax.all_to_all(outgoing, 'ep', split_axis=1, concat_axis=0, tiled=True)  29.4 us
    dot_general x2, local copies, waits for them, and re-layouts, body(): jnp.dot(jnp.concatenate(lax.all_to_all(jnp.stack([values] * lax.axis_size...  26 us
    all_to_all x1, waiting for transfers between devices, body(): lax.all_to_all(outgoing, 'ep', split_axis=1, concat_axis=0, tiled=True)  25.8 us
    reshape x1, local copies, waits for them, and re-layouts, body(): jnp.concatenate(lax.all_to_all(jnp.stack([values] * lax.axis_size('ep')),...  24 us
  transfers between devices with their start and end apart: 5, of which 5 were waited for; matrix products, arithmetic and copies ran while one was open for 2% of the time, Pallas kernels for 0%

profile of v1, /device:TPU:164, one launch (start us, length us, event | category | flops | bytes accessed | tf_op | source)
XLA Modules:
  0.0 1001.2 jit_solution(17122719681759785848)
XLA Ops:
  0.9 3.8 fusion.41
  5.5 1.7 fusion.5
  8.7 29.4 %all-to-all-start = ((bf16[4,128,512]{2,0,1:T(4,128)(2,1)}), bf16[4,128,512]{2,0,1:T(4,128)(2,1)S(1)}, u32[]{:S(2)}, u32[]{:S(2)}) async-start(bf16[4,128,512]{2,0,1:T(4,128)(2,1)} %bitcast.9), calls=%async_computation | async-start | bytes 1048576 | tf_op jit(solution)/shard_map/all_to_all | solution.py:96
  38.1 1.7 copy.54
  39.8 4.2 reshape.158
  44.1 25.8 %all-to-all-done = bf16[4,128,512]{2,0,1:T(4,128)(2,1)S(1)} async-done(((bf16[4,128,512]{2,0,1:T(4,128)(2,1)}), bf16[4,128,512]{2,0,1:T(4,128)(2,1)S(1)}, u32[]{:S(2)}, u32[]{:S(2)}) %all-to-all-start) | async-done | bytes 524320 | tf_op jit(solution)/shard_map/all_to_all | solution.py:96
  69.9 10.4 %all-to-all-start.2 = ((bf16[128,2,1792]{2,1,0:T(2,128)(2,1)}), bf16[128,2,1792]{2,1,0:T(2,128)(2,1)S(1)}, u32[]{:S(2)}, u32[]{:S(2)}) async-start(bf16[128,2,1792]{2,1,0:T(2,128)(2,1)} %reshape.158), calls=%async_computation.2 | async-start | bytes 1835008 | tf_op jit(solution)/shard_map/all_to_all | solution.py:100
  80.3 1.2 reshape.143
  81.8 46.7 %all-to-all-done.2 = bf16[128,2,1792]{2,1,0:T(2,128)(2,1)S(1)} async-done(((bf16[128,2,1792]{2,1,0:T(2,128)(2,1)}), bf16[128,2,1792]{2,1,0:T(2,128)(2,1)S(1)}, u32[]{:S(2)}, u32[]{:S(2)}) %all-to-all-start.2) | async-done | bytes 917536 | tf_op jit(solution)/shard_map/all_to_all | solution.py:100
  128.5 4.3 stack.3
  132.8 9.9 all-to-all-start.1
  142.7 2.0 reshape.159
  144.8 1.6 bitcast_bitcast_fusion
  146.4 1.8 copy.43
  148.2 3.0 reshape.154
  151.2 357.4 %all-to-all-done.1 = bf16[128,512,64]{1,2,0:T(8,128)(2,1)} async-done(((bf16[128,512,64]{1,2,0:T(8,128)(2,1)}), bf16[128,512,64]{1,2,0:T(8,128)(2,1)}, u32[]{:S(2)}, u32[]{:S(2)}) %all-to-all-start.1) | async-done | bytes 8388640 | tf_op jit(solution)/shard_map/all_to_all | solution.py:103
  508.5 24.0 %copy.41 = bf16[512,128,64]{2,1,0:T(8,128)(2,1)} copy(bf16[512,128,64]{0,2,1:T(8,128)(2,1)} %bitcast.12) | data formatting | bytes 16777216 | tf_op jit(solution)/shard_map/reshape | solution.py:102
  532.5 25.9 %dot_general.43 = bf16[128,4,8192]{2,1,0:T(4,128)(2,1)} reshape(bf16[512,128,64]{2,1,0:T(8,128)(2,1)} %copy.41) | data formatting | bytes 16777216 | tf_op jit(solution)/shard_map/dot_general | solution.py:101
  558.5 12.4 %fusion = f32[128,4,56]{0,2,1:T(8,128)S(1)} fusion(bf16[8192,56,1]{0,1,2:T(8,128)(2,1)S(1)} %reshape.154, bf16[128,4,8192]{2,1,0:T(4,128)(2,1)} %dot_general.43), kind=kOutput, calls=%fused_computation.2 | convolution fusion | flops 469762048 | bytes 9420800 | tf_op jit(solution)/shard_map/dot_general | solution.py:101
  571.9 13.0 %all-to-all-start.3 = ((f32[128,1,224]{2,1,0:T(1,128)}), f32[128,1,224]{2,1,0:T(1,128)S(1)}, u32[]{:S(2)}, u32[]{:S(2)}) async-start(f32[128,1,224]{2,1,0:T(1,128)} %reshape.160), calls=%async_computation.3 | async-start | bytes 262144 | tf_op jit(solution)/shard_map/all_to_all | solution.py:108
  585.5 14.2 %all-to-all-done.3 = f32[128,1,224]{2,1,0:T(1,128)S(1)} async-done(((f32[128,1,224]{2,1,0:T(1,128)}), f32[128,1,224]{2,1,0:T(1,128)S(1)}, u32[]{:S(2)}, u32[]{:S(2)}) %all-to-all-start.3) | async-done | bytes 114720 | tf_op jit(solution)/shard_map/all_to_all | solution.py:108
  603.1 1.2 convolution_convert_fusion.1
  604.2 3.8 copy.49
  608.0 176.9 %all_to_all.65 = bf16[128,2,7168]{2,1,0:T(2,128)(2,1)} all-to-all(bf16[128,2,7168]{2,1,0:T(2,128)(2,1)S(1)} %copy.49), channel_id=1, replica_groups=mesh['rep'=2,'ep'=128] {'ep'}, dimensions={0} | all-to-all | bytes 7340032 | tf_op jit(solution)/shard_map/all_to_all | solution.py:133
  784.9 8.4 reshape.145
  793.3 3.7 fusion.43
  797.1 6.6 convolution_convert_fusion
  803.6 8.1 convert_element_type.95
  811.8 10.9 %all-to-all-start.5 = ((bf16[128,2,7168]{2,1,0:T(2,128)(2,1)}), bf16[128,2,7168]{2,1,0:T(2,128)(2,1)}, u32[]{:S(2)}, u32[]{:S(2)}) async-start(bf16[128,2,7168]{2,1,0:T(2,128)(2,1)} %convert_element_type.95), calls=%async_computation.5 | async-start | bytes 7340032 | tf_op jit(solution)/shard_map/all_to_all | solution.py:137
  822.8 165.5 %all-to-all-done.5 = bf16[128,2,7168]{2,1,0:T(2,128)(2,1)} async-done(((bf16[128,2,7168]{2,1,0:T(2,128)(2,1)}), bf16[128,2,7168]{2,1,0:T(2,128)(2,1)}, u32[]{:S(2)}, u32[]{:S(2)}) %all-to-all-start.5) | async-done | bytes 3670048 | tf_op jit(solution)/shard_map/all_to_all | solution.py:137
  988.3 8.4 reshape.146
  996.7 3.6 fusion.2
  (63 shorter events, 9.0 us)
Async XLA Ops:
  0.0 797.0 %copy-start = (bf16[128,7168]{1,0:T(8,128)(2,1)S(1)}, bf16[128,7168]{1,0:T(8,128)(2,1)}, u32[]{:S(2)}) copy-start(bf16[128,7168]{1,0:T(8,128)(2,1)} %param.27) | copy-start | bytes 5505028
  0.9 3.8 copy-start.2
  0.9 3.8 copy-start.10
  0.9 4.6 copy-start.1
  7.2 30.9 %copy-start.4 = (bf16[64,7168]{1,0:T(8,128)(2,1)S(1)}, bf16[64,7168]{1,0:T(8,128)(2,1)}, u32[]{:S(2)}) copy-start(bf16[64,7168]{1,0:T(8,128)(2,1)} %param.20) | copy-start | bytes 2752516
  8.7 61.2 %all-to-all-start = ((bf16[4,128,512]{2,0,1:T(4,128)(2,1)}), bf16[4,128,512]{2,0,1:T(4,128)(2,1)S(1)}, u32[]{:S(2)}, u32[]{:S(2)}) async-start(bf16[4,128,512]{2,0,1:T(4,128)(2,1)} %bitcast.9), calls=%async_computation | async-start | bytes 1048576 | tf_op jit(solution)/shard_map/all_to_all | solution.py:96
  38.1 43.4 %copy-start.7 = (bf16[512,64]{0,1:T(8,128)(2,1)S(1)}, bf16[512,64]{0,1:T(8,128)(2,1)}, u32[]{:S(2)}) copy-start(bf16[512,64]{0,1:T(8,128)(2,1)} %param.19) | copy-start | bytes 196612
  69.9 10.4 %copy-start.3 = (bf16[4,128,512]{2,0,1:T(4,128)(2,1)}, bf16[4,128,512]{2,0,1:T(4,128)(2,1)S(1)}, u32[]{:S(2)}) copy-start(bf16[4,128,512]{2,0,1:T(4,128)(2,1)S(1)} %all-to-all-done) | copy-start | bytes 1572868
  69.9 58.6 %all-to-all-start.2 = ((bf16[128,2,1792]{2,1,0:T(2,128)(2,1)}), bf16[128,2,1792]{2,1,0:T(2,128)(2,1)S(1)}, u32[]{:S(2)}, u32[]{:S(2)}) async-start(bf16[128,2,1792]{2,1,0:T(2,128)(2,1)} %reshape.158), calls=%async_computation.2 | async-start | bytes 1835008 | tf_op jit(solution)/shard_map/all_to_all | solution.py:100
  132.8 375.7 %all-to-all-start.1 = ((bf16[128,512,64]{1,2,0:T(8,128)(2,1)}), bf16[128,512,64]{1,2,0:T(8,128)(2,1)}, u32[]{:S(2)}, u32[]{:S(2)}) async-start(bf16[128,512,64]{1,2,0:T(8,128)(2,1)} %stack.3), calls=%async_computation.1 | async-start | bytes 16777216 | tf_op jit(solution)/shard_map/all_to_all | solution.py:103
  558.4 26.6 %copy-start.6 = (bf16[2,2,7168]{2,1,0:T(2,128)(2,1)S(1)}, bf16[2,2,7168]{2,1,0:T(2,128)(2,1)}, u32[]{:S(2)}) copy-start(bf16[2,2,7168]{2,1,0:T(2,128)(2,1)} %param.18) | copy-start | bytes 172036
  558.4 26.8 %copy-start.8 = (bf16[7168]{0:T(1024)(128)(2,1)S(1)}, bf16[7168]{0:T(1024)(128)(2,1)}, u32[]{:S(2)}) copy-start(bf16[7168]{0:T(1024)(128)(2,1)} %param.21) | copy-start | bytes 43012
  558.4 26.9 %copy-start.11 = (s32[2,2,8]{2,1,0:T(2,128)S(1)}, s32[2,2,8]{2,1,0:T(2,128)}, u32[]{:S(2)}) copy-start(s32[2,2,8]{2,1,0:T(2,128)} %param.24) | copy-start | bytes 388
  558.5 27.0 %copy-start.9 = (s32[2,2,8]{2,1,0:T(2,128)S(1)}, s32[2,2,8]{2,1,0:T(2,128)}, u32[]{:S(2)}) copy-start(s32[2,2,8]{2,1,0:T(2,128)} %param.23) | copy-start | bytes 388
  570.8 31.0 %copy-start.5 = (bf16[7168,16]{0,1:T(8,128)(2,1)S(1)}, bf16[7168,16]{0,1:T(8,128)(2,1)}, u32[]{:S(2)}) copy-start(bf16[7168,16]{0,1:T(8,128)(2,1)} %param.22) | copy-start | bytes 688132
  571.9 27.8 %all-to-all-start.3 = ((f32[128,1,224]{2,1,0:T(1,128)}), f32[128,1,224]{2,1,0:T(1,128)S(1)}, u32[]{:S(2)}, u32[]{:S(2)}) async-start(f32[128,1,224]{2,1,0:T(1,128)} %reshape.160), calls=%async_computation.3 | async-start | bytes 262144 | tf_op jit(solution)/shard_map/all_to_all | solution.py:108
  811.8 176.5 %all-to-all-start.5 = ((bf16[128,2,7168]{2,1,0:T(2,128)(2,1)}), bf16[128,2,7168]{2,1,0:T(2,128)(2,1)}, u32[]{:S(2)}, u32[]{:S(2)}) async-start(bf16[128,2,7168]{2,1,0:T(2,128)(2,1)} %convert_element_type.95), calls=%async_computation.5 | async-start | bytes 7340032 | tf_op jit(solution)/shard_map/all_to_all | solution.py:137
